TPU v7x, 32 devices: a whole 2x2x4 slice. The times are simulated.
32 devices in a mesh: freq: 8 (over z, y), rows: 4 (over x, core).
Axes of the slice: x: 2, y: 2, z: 4, core: 2. Of those that a mesh axis runs over, the one named last changes fastest.
Arguments:
- wavefield: bfloat16 [10240, 32, 1024], P('freq', 'rows'), may hold values from -6 to 6
- u_factors: bfloat16 [2, 16, 4, 256, 512], P(None, 'freq', 'rows'), may hold values from -0.25 to 0.25
- v_factors: bfloat16 [2, 16, 4, 512, 256], P(None, 'freq', 'rows'), may hold values from -0.375 to 0.375
- tile_ranks: int32 [16, 4, 40], P('freq', 'rows'), may hold values from 1 to 64, as said below
- tile_offsets: int32 [16, 4, 40], P('freq', 'rows'), may hold values from 0 to 511, as said below
Outputs:
- convolved: bfloat16 [1024, 32, 1024], P(('rows', 'freq'))
Inputs may be any that keep to these rules, and one draw needn't show every extreme that they name: tile_ranks[k, i, j] is the rank of tile (i, j) of frequency k; the ranks of one tile row sum to at most 512, exactly 512 on some row of every draw, and every tile row has a tile of rank 64. tile_offsets[k, i, j] is the sum of tile_ranks[k, i, j2] over j2 < j.
All inputs are finite; a program needn't handle non-finite values.
Results may differ from a plain program's by a relative error of at most 0.0072.
Values may be sent and summed in bfloat16 or wider, within the bound.
No kernel may reach another device: no remote copies, remote signals or barrier semaphores. Data moves between devices by JAX's collectives and lax.ppermute only.
A program may use at most 128 MiB of HBM per device.

v0:
```python
import functools
import math

import jax
import jax.numpy as jnp
from jax import lax
from jax.experimental import pallas as pl
from jax.experimental.pallas import tpu as pltpu
from jax.sharding import PartitionSpec as P


RANK_MAX = 64
LANES = 128
SUBLANES = 8
NT = (((1,), (1,)), ((), ()))
VMEM = pl.BlockSpec(memory_space=pltpu.VMEM)
SMEM = pl.BlockSpec(memory_space=pltpu.SMEM)
PAIRED = (4, 8, 16)
AHEAD = 3


def spectral_tables(freq_count, sample_count):
    freq_bins = jnp.arange(freq_count, dtype=jnp.int32) + 1
    sample_index = jnp.arange(sample_count, dtype=jnp.int32)
    phase_int = freq_bins[:, None] * sample_index[None, :] % sample_count
    angles = phase_int.astype(jnp.float32) * (2.0 * math.pi / sample_count)
    cosine = jnp.cos(angles)
    minus_sine = -jnp.sin(angles)
    stacked = jnp.stack([cosine, minus_sine], axis=1)
    forward = (stacked / math.sqrt(sample_count)).astype(jnp.bfloat16)
    inverse = (stacked / math.sqrt(freq_count)).astype(jnp.bfloat16)
    return (forward, inverse)


def tile_windows(v_row, u_row, starts, rank_max):
    columns = starts.shape[0]
    slot_index = (starts[:, None] + jnp.arange(rank_max, dtype=jnp.int32)[None, :]).reshape(-1)
    v_padded = jnp.pad(v_row, ((0, 0), (0, rank_max), (0, 0)))
    u_padded = jnp.pad(u_row, ((0, 0), (0, 0), (0, rank_max)))
    v_win = jnp.take(v_padded, slot_index, axis=1).reshape(2, columns, rank_max, v_row.shape[2])
    u_win = jnp.take(u_padded, slot_index, axis=2).reshape(2, u_row.shape[1], columns, rank_max)
    return (v_win, u_win)


def slot_lookup(starts, counts, rank_max, slot_count):
    position = jnp.arange(slot_count, dtype=jnp.int32)
    started = starts[:, None, :] <= position[None, :, None]
    owner_tile = jnp.sum(started.astype(jnp.int32), axis=2) - 1
    first_slot = jnp.max(jnp.where(started, starts[:, None, :], 0), axis=2)
    within = position[None, :] - first_slot
    live_slot = position[None, :] < (starts[:, -1] + counts[:, -1])[:, None]
    flat_index = jnp.where(live_slot, owner_tile * rank_max + within, 0)
    return (flat_index, live_slot)


def take_slots(values, chosen):
    return jnp.take(values, chosen, axis=1)


def per_device(wavefield, u_factors, v_factors, tile_ranks, tile_offsets):
    rec_dev, src_dev, samples = wavefield.shape
    freq_dev = u_factors.shape[1]
    rows_dev = u_factors.shape[2]
    tile_size = u_factors.shape[3]
    slot_count = u_factors.shape[4]
    freq_group = lax.axis_size("freq")
    row_group = lax.axis_size("rows")
    freqs = freq_dev * freq_group
    receivers = rec_dev * freq_group
    columns = receivers // tile_size
    sources = src_dev * row_group
    forward, inverse = spectral_tables(freqs, samples)
    spectrum = jnp.einsum("kct,rst->kcrs", forward, wavefield, preferred_element_type=jnp.float32)
    spectrum = spectrum.astype(jnp.bfloat16).reshape(freqs, 2, rec_dev * src_dev)
    windows = jax.vmap(
        functools.partial(tile_windows, rank_max=RANK_MAX), in_axes=(1, 1, 0), out_axes=(1, 1)
    )
    rank_slots = jnp.arange(RANK_MAX, dtype=jnp.int32)
    tile_row = 0
    v_win, u_win = windows(
        v_factors[:, :, tile_row], u_factors[:, :, tile_row], tile_offsets[:, tile_row]
    )
    rank_mask = rank_slots[None, None, :] < tile_ranks[:, tile_row, :, None]
    flat_index, live_slot = slot_lookup(
        tile_offsets[:, tile_row], tile_ranks[:, tile_row], RANK_MAX, slot_count
    )
    prepared = [(v_win, u_win, rank_mask, flat_index, live_slot)]
    by_frequency = lax.all_to_all(spectrum, "freq", split_axis=0, concat_axis=2, tiled=True)
    portion = lax.all_gather(by_frequency[None], "rows", axis=0, tiled=True)
    blocks_in = portion.shape[0]
    spectra = portion.reshape(blocks_in, freq_dev, 2, columns, tile_size, src_dev)
    spectra = jnp.transpose(spectra, (1, 2, 3, 4, 0, 5)).reshape(
        freq_dev, 2, columns, tile_size, blocks_in * src_dev
    )
    tile_row = 0
    v_win, u_win, rank_mask, flat_index, live_slot = prepared[tile_row]
    quadrants = jnp.einsum(
        "afjmr,fbjrs->fabjms", v_win, spectra, preferred_element_type=jnp.float32
    )
    coeffs = jnp.stack(
        [quadrants[:, 0, 0] - quadrants[:, 1, 1], quadrants[:, 0, 1] + quadrants[:, 1, 0]], axis=1
    )
    coeffs = jnp.where(rank_mask[:, None, :, :, None], coeffs, 0.0).astype(jnp.bfloat16)
    stacked = coeffs.reshape(freq_dev, 2, columns * RANK_MAX, blocks_in * src_dev)
    packed = jax.vmap(take_slots)(stacked, flat_index)
    packed = jnp.where(live_slot[:, None, :, None], packed, jnp.zeros((), jnp.bfloat16))
    products = jnp.einsum(
        "afrk,fcks->facrs", u_factors[:, :, tile_row], packed, preferred_element_type=jnp.float32
    )
    results = [
        jnp.stack(
            [products[:, 0, 0] - products[:, 1, 1], products[:, 0, 1] + products[:, 1, 0]], axis=1
        )
    ]
    merged = jnp.stack(results, axis=2)
    bands = merged.astype(jnp.bfloat16).reshape(
        freq_dev, 2, rows_dev * tile_size, blocks_in, src_dev
    )
    bands = bands.reshape(freq_dev, 2, rows_dev * tile_size * sources)
    returned = lax.all_to_all(bands, "freq", split_axis=2, concat_axis=0, tiled=True)
    series = jnp.einsum("kcq,kct->qt", returned, inverse, preferred_element_type=jnp.float32)
    return series.astype(jnp.bfloat16).reshape(rows_dev * tile_size // freq_group, sources, samples)


def cosines(kinds, samples):
    row = lax.broadcasted_iota(jnp.int32, (kinds, samples), 0)
    index = lax.broadcasted_iota(jnp.int32, (kinds, samples), 1)
    phase = (((row >> 1) + 1) * index + (row & 1) * (samples // 4)) & (samples - 1)
    angles = phase.astype(jnp.float32) * (2.0 * math.pi / samples)
    return (jnp.cos(angles) * (1.0 / math.sqrt(samples))).astype(jnp.bfloat16)


def transform_kernel(traces_ref, *refs):
    groups = lax.axis_size("freq")
    outs, (table_ref, traces, sems, repeated, products, turned) = refs[:groups], refs[groups:]
    me = lax.axis_index("freq")
    rows = products.shape[1]
    kinds = turned.shape[0] // SUBLANES
    packs = LANES // kinds
    blocks = traces_ref.shape[0] // rows
    each = outs[0].shape[0]

    def copy(i):
        part = pl.ds(pl.multiple_of(i * rows, rows), rows)
        return pltpu.make_async_copy(traces_ref.at[part, :], traces.at[part, :], sems.at[i])

    def turn(i, source_rows):
        place = lax.broadcasted_iota(jnp.int32, (rows // SUBLANES, LANES), 1) // kinds
        for first in range(0, SUBLANES, packs):
            mixed = source_rows[pl.ds(first, rows // SUBLANES, stride=SUBLANES), :]
            for m in range(1, packs):
                part = source_rows[pl.ds(first + m, rows // SUBLANES, stride=SUBLANES), :]
                mixed = jnp.where(place == m, part, mixed)
            mixed = mixed.T
            for m in range(packs):
                turned[pl.ds(first + m, kinds, stride=SUBLANES), :] = mixed[
                    m * kinds : (m + 1) * kinds
                ]
        lanes = pl.ds(pl.multiple_of(i * LANES, LANES), LANES)
        for shift, out in enumerate(outs):
            group = me ^ shift
            start = pl.multiple_of(group * each, each)
            out[:, lanes] = turned[pl.ds(start, each), :].astype(jnp.bfloat16)

    for i in range(min(AHEAD, blocks)):
        copy(i).start()
    table_ref[...] = cosines(kinds, traces.shape[1])
    for m in range(packs):
        repeated[m * kinds : (m + 1) * kinds, :] = table_ref[...]

    def step(i, carry):
        now = lax.rem(i, 2)

        @pl.when(i + AHEAD < blocks)
        def _():
            copy(i + AHEAD).start()

        copy(i).wait()
        part = pl.ds(pl.multiple_of(i * rows, rows), rows)
        turn(jnp.maximum(i - 1, 0), products.at[1 - now])
        products[now] = lax.dot_general(
            traces[part, :], repeated[...], NT, preferred_element_type=jnp.float32
        )
        return carry

    lax.fori_loop(0, blocks, step, 0)
    turn(blocks - 1, products.at[(blocks - 1) % 2])


def transform(traces, kinds, groups):
    rows, samples = traces.shape
    receivers = rows // SUBLANES
    shape = jax.ShapeDtypeStruct((kinds * SUBLANES // groups, receivers), jnp.bfloat16)
    return pl.pallas_call(
        transform_kernel,
        in_specs=[pl.BlockSpec(memory_space=pltpu.HBM)],
        out_specs=[VMEM] * (groups + 1),
        out_shape=[shape] * groups + [jax.ShapeDtypeStruct((kinds, samples), jnp.bfloat16)],
        scratch_shapes=[
            pltpu.VMEM((rows, samples), jnp.bfloat16),
            pltpu.SemaphoreType.DMA((receivers // LANES,)),
            pltpu.VMEM((LANES, samples), jnp.bfloat16),
            pltpu.VMEM((2, LANES * SUBLANES, LANES), jnp.float32),
            pltpu.VMEM((kinds * SUBLANES, LANES), jnp.float32),
        ],
        compiler_params=pltpu.CompilerParams(vmem_limit_bytes=48 * 2**20),
        cost_estimate=pl.CostEstimate(
            flops=2 * rows * samples * 256, bytes_accessed=rows * samples * 2, transcendentals=0
        ),
        name="transform",
    )(traces)


def coefficient_kernel(shifts, sides, before, *refs):
    count = len(shifts)
    refs = list(refs)
    offsets = [refs.pop(0) for _ in range(sides)]
    own = [refs.pop(0) for _ in range(count)]
    twin = [refs.pop(0) for _ in range(count)]
    factors = [refs.pop(0) for _ in range(sides)]
    earlier = [refs.pop(0) for _ in range(before)]
    outs = [refs.pop(0) for _ in range(sides)]
    (lhs,) = refs
    groups = lax.axis_size("freq")
    me = lax.axis_index("freq")
    core = lax.rem(lax.axis_index("rows"), 2)
    _, freqs, slots, tile = factors[0].shape
    per_block = own[0].shape[1] // tile
    columns = groups * per_block
    half = 2 * SUBLANES
    deep = 2 * half
    for k in range(freqs):
        for arrays, at in ((own, core), (twin, 1 - core)):
            for b in range(count):
                for inner in range(per_block):
                    start = (b * per_block + inner) * deep + at * half
                    lhs[k, pl.ds(pl.multiple_of(start, half), half), :] = arrays[b][
                        k * half : (k + 1) * half, inner * tile : (inner + 1) * tile
                    ]
    for side in range(sides):
        for k in range(freqs):
            for low in range(0, slots, tile):
                slot = lax.broadcasted_iota(jnp.int32, (deep, tile), 1) + low
                chosen = []
                for part in range(2):
                    products = lax.dot_general(
                        lhs[k],
                        factors[side][part, k, low : low + tile, :],
                        NT,
                        preferred_element_type=jnp.float32,
                    )
                    total = jnp.zeros((deep, tile), jnp.float32)
                    for b, shift in enumerate(shifts):
                        column = (me ^ shift) * per_block
                        value = total
                        for inner in range(per_block):
                            at = (b * per_block + inner) * deep
                            value = jnp.where(
                                slot >= offsets[side][k, 0, column + inner],
                                products[at : at + deep],
                                value,
                            )
                        after = jnp.minimum(column + per_block, columns - 1)
                        end = jnp.where(
                            column + per_block < columns, offsets[side][k, 0, after], slots
                        )
                        total = jnp.where(slot >= end, total, value)
                    chosen.append(total)
                by_real, by_imag = chosen
                n = SUBLANES
                real = [by_real[g : g + n] - by_imag[g + n : g + 2 * n] for g in (0, half)]
                imag = [by_real[g + n : g + 2 * n] + by_imag[g : g + n] for g in (0, half)]
                for c, pieces in enumerate((real, imag)):
                    value = jnp.concatenate(pieces, 0)
                    if side < before:
                        value += earlier[side][k, c, :, low : low + tile].astype(jnp.float32)
                    outs[side][k, c, :, low : low + tile] = value.astype(jnp.bfloat16)


def coefficients(shifts, offsets, own, twin, factors, earlier=()):
    sides, count = len(offsets), len(shifts)
    _, freqs, slots, tile = factors[0].shape
    columns = count * own[0].shape[1] // tile
    shape = jax.ShapeDtypeStruct((freqs, 2, 2 * SUBLANES, slots), jnp.bfloat16)
    return pl.pallas_call(
        functools.partial(coefficient_kernel, tuple(shifts), sides, len(earlier)),
        in_specs=[SMEM] * sides + [VMEM] * (2 * count + sides + len(earlier)),
        out_specs=[VMEM] * sides,
        out_shape=[shape] * sides,
        scratch_shapes=[pltpu.VMEM((freqs, columns * 4 * SUBLANES, tile), jnp.bfloat16)],
        compiler_params=pltpu.CompilerParams(vmem_limit_bytes=16 * 2**20),
        cost_estimate=pl.CostEstimate(
            flops=2 * 2 * sides * freqs * slots * columns * 4 * SUBLANES * tile,
            bytes_accessed=2**20,
            transcendentals=0,
        ),
        name="coefficients",
    )(*offsets, *own, *twin, *factors, *earlier)


def band_kernel(add, at_near, offsets_ref, ranks_ref, coeffs_ref, u_ref, *refs):
    refs = list(refs)
    other_ref = refs.pop(0) if add else None
    out_ref, rhs, crossed = refs[:3]
    freqs, _, sources, slots = coeffs_ref.shape
    tile = u_ref.shape[2]
    place = lax.rem(lax.axis_index("rows") // 2, 2)
    at = place if at_near else 1 - place
    last = offsets_ref.shape[2] - 1
    wide = 2 * sources
    rhs[...] = jnp.zeros_like(rhs)
    crossed[...] = jnp.zeros_like(crossed)
    slot = lax.broadcasted_iota(jnp.int32, (sources, slots), 1)
    for k in range(freqs):
        live = slot < offsets_ref[k, 0, last] + ranks_ref[k, 0, last]
        for part in range(2):
            value = jnp.where(live, coeffs_ref[k, part].astype(jnp.float32), 0.0)
            start = pl.multiple_of((2 * k + part) * wide + at * sources, sources)
            rhs[k, pl.ds(start, sources), :] = value.astype(jnp.bfloat16)
            start = pl.multiple_of((2 * k + 1 - part) * wide + at * sources, sources)
            value = value if part == 0 else -value
            crossed[k, pl.ds(start, sources), :] = value.astype(jnp.bfloat16)
    total = other_ref[...] if add else jnp.zeros((tile, 2 * freqs * wide), jnp.float32)
    for k in range(freqs):
        for part, ref in enumerate((rhs, crossed)):
            total += lax.dot_general(u_ref[part, k], ref[k], NT, preferred_element_type=jnp.float32)
    if not add:
        out_ref[...] = total
        return
    bands, mix = refs[3:]
    groups = out_ref.shape[0]
    bands[...] = total
    packs = LANES // wide
    kinds = 2 * freqs
    block = lax.broadcasted_iota(jnp.int32, (tile // packs, LANES), 1) // wide
    loaded = [bands[pl.ds(b, tile // packs, stride=packs), :] for b in range(packs)]
    rows = tile // packs // groups
    for kind in range(kinds):
        mixed = jnp.zeros((tile // packs, LANES), jnp.float32)
        for b in range(packs):
            shift = (b - kind) * wide % LANES
            moved = pltpu.roll(loaded[b], shift, 1) if shift else loaded[b]
            mixed = jnp.where(block == b, moved, mixed)
        mix[:, kind * rows : (kind + 1) * rows, :] = mixed.reshape(groups, rows, LANES)
    out_ref[...] = mix[...].astype(jnp.bfloat16)


def bands_of(at_near, offsets, ranks, coeffs, u_own, groups, other=None):
    add = other is not None
    freqs, _, sources, slots = coeffs.shape
    tile = u_own.shape[2]
    rows = 2 * freqs * tile * 2 * sources // LANES // groups
    partial = jax.ShapeDtypeStruct((tile, LANES), jnp.float32)
    whole = jax.ShapeDtypeStruct((groups, rows, LANES), jnp.bfloat16)
    spread = pltpu.VMEM((freqs, LANES, slots), jnp.bfloat16)
    mixing = [pltpu.VMEM((tile, LANES), jnp.float32), pltpu.VMEM(whole.shape, jnp.float32)]
    return pl.pallas_call(
        functools.partial(band_kernel, add, at_near),
        in_specs=[SMEM] * 2 + [VMEM] * (3 if add else 2),
        out_specs=VMEM,
        out_shape=whole if add else partial,
        scratch_shapes=[spread, spread] + (mixing if add else []),
        compiler_params=pltpu.CompilerParams(vmem_limit_bytes=8 * 2**20),
        cost_estimate=pl.CostEstimate(
            flops=2 * 2 * freqs * tile * LANES * slots, bytes_accessed=2**20, transcendentals=0
        ),
        name="bands",
    )(offsets, ranks, coeffs, u_own, *([other] if add else []))


def series_kernel(scale, bands_ref, table_ref, out_ref, wide, done, sems):
    groups, rows, lanes = bands_ref.shape
    kinds = table_ref.shape[0]
    steps = groups * rows // kinds
    wide[...] = bands_ref[...].astype(jnp.float32).reshape(groups * rows, lanes) * scale
    copies = []
    for i in range(steps):
        part = wide[pl.ds(i, kinds, stride=steps), :]
        done[i] = jnp.dot(
            part.T.astype(jnp.bfloat16), table_ref[...], preferred_element_type=jnp.float32
        ).astype(jnp.bfloat16)
        copies.append(
            pltpu.make_async_copy(
                done.at[i], out_ref.at[i * lanes : (i + 1) * lanes, :], sems.at[i]
            )
        )
        copies[-1].start()
    for copy in copies:
        copy.wait()


def series_of(bands, table, scale):
    groups, rows, lanes = bands.shape
    kinds, samples = table.shape
    steps = groups * rows // kinds
    return pl.pallas_call(
        functools.partial(series_kernel, scale),
        in_specs=[VMEM] * 2,
        out_specs=pl.BlockSpec(memory_space=pl.ANY),
        out_shape=jax.ShapeDtypeStruct((steps * lanes, samples), jnp.bfloat16),
        scratch_shapes=[
            pltpu.VMEM((groups * rows, lanes), jnp.float32),
            pltpu.VMEM((steps, lanes, samples), jnp.bfloat16),
            pltpu.SemaphoreType.DMA((steps,)),
        ],
        compiler_params=pltpu.CompilerParams(vmem_limit_bytes=16 * 2**20),
        cost_estimate=pl.CostEstimate(
            flops=2 * steps * lanes * kinds * samples,
            bytes_accessed=steps * lanes * samples * 2,
            transcendentals=0,
        ),
        name="series",
    )(bands, table)


def fits(rec_dev, src_dev, samples, freq_dev, rows_dev, tile, slots, freq_group, row_group):
    kinds = 2 * freq_dev * freq_group
    ratio = math.sqrt(samples) / math.sqrt(freq_dev * freq_group)
    return (
        math.frexp(ratio)[0] == 0.5
        and math.sqrt(samples).is_integer()
        and samples & (samples - 1) == 0
        and src_dev == SUBLANES
        and row_group == 4
        and rows_dev == 1
        and freq_group in PAIRED
        and rec_dev % tile == 0
        and tile % (2 * LANES) == 0
        and slots % tile == 0
        and LANES % kinds == 0
        and SUBLANES % (LANES // kinds) == 0
        and 2 * freq_dev * src_dev * row_group == LANES
        and tile % (4 * SUBLANES * freq_group) == 0
    )


def shift_order(groups):
    return [(groups // 2 - 1 - 2 * i) % (groups - 1) + 1 for i in range(groups - 1)]


def arrivals(groups):
    order = shift_order(groups)
    crossing = [s for s in order[1:] if s >= groups // 2]
    early = [s for s in order if s not in crossing and s != 1]
    return [0] + early, [1] + crossing[:-2], crossing[-2:]


def per_device_fast(wavefield, u_factors, v_factors, tile_ranks, tile_offsets):
    rec_dev, src_dev, samples = wavefield.shape
    freq_dev = u_factors.shape[1]
    groups = lax.axis_size("freq")
    row_group = lax.axis_size("rows")
    freqs = freq_dev * groups
    sources = src_dev * row_group
    tile = u_factors.shape[3]
    across = [(i, i ^ 2) for i in range(row_group)]
    beside = [(i, i ^ 1) for i in range(row_group)]
    u_own, v_own = u_factors[:, :, 0], v_factors[:, :, 0]
    v_far = lax.ppermute(v_own, "rows", across)
    offsets_far = lax.ppermute(tile_offsets, "rows", across)
    *sent, table = transform(wavefield.reshape(rec_dev * src_dev, samples), 2 * freqs, groups)
    own = {0: sent[0]}
    for shift in shift_order(groups):
        swap = [(i, i ^ shift) for i in range(groups)]
        own[shift] = lax.ppermute(sent[shift], "freq", swap)
    early, middle, last = arrivals(groups)

    def twins(shifts):
        pairs = {}
        for shift in shifts:
            pairs[shift] = lax.ppermute(own[shift], "rows", beside)
        return pairs

    def blocks(shifts):
        return [own[s] for s in shifts], [twin[s] for s in shifts]

    twin = twins(early)
    (near,) = coefficients(early, [tile_offsets], *blocks(early), [v_own])
    waiting, near = lax.optimization_barrier(([own[s] for s in middle], near))
    own.update(zip(middle, waiting))
    twin.update(twins(middle))
    (leaving,) = coefficients(early, [offsets_far], *blocks(early), [v_far])
    waiting, near, leaving = lax.optimization_barrier(([own[s] for s in last], near, leaving))
    own.update(zip(last, waiting))
    twin.update(twins(last))
    (leaving,) = coefficients(middle, [offsets_far], *blocks(middle), [v_far], [leaving])
    (leaving,) = coefficients(last, [offsets_far], *blocks(last), [v_far], [leaving])
    late = middle + last
    far = lax.ppermute(leaving, "rows", across)
    (near,) = coefficients(late, [tile_offsets], *blocks(late), [v_own], [near])
    half = bands_of(True, tile_offsets, tile_ranks, near, u_own, groups)
    bands = bands_of(False, tile_offsets, tile_ranks, far, u_own, groups, half)
    returned = lax.all_to_all(bands, "freq", split_axis=0, concat_axis=0, tiled=True)
    series = series_of(returned, table, math.sqrt(samples) / math.sqrt(freqs))
    return series.reshape(tile // groups, sources, samples)


def choose(wavefield, u_factors, v_factors, tile_ranks, tile_offsets):
    ok = fits(
        wavefield.shape[0],
        wavefield.shape[1],
        wavefield.shape[2],
        u_factors.shape[1],
        u_factors.shape[2],
        u_factors.shape[3],
        u_factors.shape[4],
        lax.axis_size("freq"),
        lax.axis_size("rows"),
    )
    step = per_device_fast if ok else per_device
    return step(wavefield, u_factors, v_factors, tile_ranks, tile_offsets)


def solution(mesh):
    placed = (
        P("freq", "rows", None),
        P(None, "freq", "rows", None, None),
        P(None, "freq", "rows", None, None),
        P("freq", "rows", None),
        P("freq", "rows", None),
    )
    return jax.shard_map(
        choose,
        mesh=mesh,
        in_specs=placed,
        out_specs=P(("rows", "freq"), None, None),
        check_vma=False,
    )
```

profile of v0, /device:TPU:0, one launch (start us, length us, event | category | flops | bytes accessed | tf_op | source)
XLA Modules:
  0.0 57.8 jit_solution(949615942581021499)
XLA Ops:
  0.0 3.0 %collective-permute-start.12 = (bf16[2,2,512,256]{3,2,1,0:T(8,128)(2,1)}, bf16[2,2,512,256]{3,2,1,0:T(8,128)(2,1)S(1)}, u32[]{:S(2)}, u32[]{:S(2)}) collective-permute-start(bf16[2,2,512,256]{3,2,1,0:T(8,128)(2,1)} %bitcast.6), channel_id=1, source_target_pairs={{0,2},{1,3},{2,0},{3,1},{4,6},{5,7},{6,4},{7,5},{8,10},{9,11},{10,... | collective-permute-start | bytes 3145736 | tf_op jit(solution)/shard_map/ppermute | solution.py:459
  3.1 9.6 %transform.1 = (bf16[32,1280]{1,0:T(8,128)(2,1)S(1)}, bf16[32,1280]{1,0:T(8,128)(2,1)S(1)}, bf16[32,1280]{1,0:T(8,128)(2,1)S(1)}, bf16[32,1280]{1,0:T(8,128)(2,1...) custom-call(bf16[10240,1024]{1,0:T(8,128)(2,1)} %bitcast.9), custom_call_target="tpu_custom_call" | custom-call | flops 5368709120 | bytes 20971520 | tf_op jit(solution)/shard_map/transform/pallas_call | solution.py:194
  12.7 1.6 %collective-permute-start.6 = (bf16[32,1280]{1,0:T(8,128)(2,1)S(1)}, bf16[32,1280]{1,0:T(8,128)(2,1)S(1)}, u32[]{:S(2)}, u32[]{:S(2)}) collective-permute-start(bf16[32,1280]{1,0:T(8,128)(2,1)S(1)} %get-tuple-element.27), channel_id=1, source_target_pairs={{0,8},{4,12},{8,0},{12,4},{16,24},{20,28},{24,16},{28,20},{1,9},{5... | collective-permute-start | bytes 245768 | tf_op jit(solution)/shard_map/ppermute | solution.py:465
  14.3 1.4 %collective-permute-start.7 = (bf16[32,1280]{1,0:T(8,128)(2,1)S(1)}, bf16[32,1280]{1,0:T(8,128)(2,1)S(1)}, u32[]{:S(2)}, u32[]{:S(2)}) collective-permute-start(bf16[32,1280]{1,0:T(8,128)(2,1)S(1)} %get-tuple-element.28), channel_id=1, source_target_pairs={{0,12},{4,8},{8,4},{12,0},{16,28},{20,24},{24,20},{28,16},{1,13},{... | collective-permute-start | bytes 245768 | tf_op jit(solution)/shard_map/ppermute | solution.py:465
  15.7 2.6 %collective-permute-start.5 = (bf16[32,1280]{1,0:T(8,128)(2,1)S(1)}, bf16[32,1280]{1,0:T(8,128)(2,1)S(1)}, u32[]{:S(2)}, u32[]{:S(2)}) collective-permute-start(bf16[32,1280]{1,0:T(8,128)(2,1)S(1)} %get-tuple-element.26), channel_id=1, source_target_pairs={{0,16},{4,20},{8,24},{12,28},{16,0},{20,4},{24,8},{28,12},{1,17},{... | collective-permute-start | bytes 245768 | tf_op jit(solution)/shard_map/ppermute | solution.py:465
  18.3 0.0 collective-permute-start.8
  18.3 0.0 collective-permute-done.6.refs_3_
  18.3 2.0 %collective-permute-start.3 = (bf16[32,1280]{1,0:T(8,128)(2,1)S(1)}, bf16[32,1280]{1,0:T(8,128)(2,1)S(1)}, u32[]{:S(2)}, u32[]{:S(2)}) collective-permute-start(bf16[32,1280]{1,0:T(8,128)(2,1)S(1)} %get-tuple-element.23), channel_id=1, source_target_pairs={{0,4},{4,0},{8,12},{12,8},{16,20},{20,16},{24,28},{28,24},{1,5},{5... | collective-permute-start | bytes 245768 | tf_op jit(solution)/shard_map/ppermute | solution.py:465
  20.3 1.2 %collective-permute-done.7.refs_4_ = bf16[32,1280]{1,0:T(8,128)(2,1)S(1)} collective-permute-done((bf16[32,1280]{1,0:T(8,128)(2,1)S(1)}, bf16[32,1280]{1,0:T(8,128)(2,1)S(1)}, u32[]{:S(2)}, u32[]{:S(2)}) %collective-permute-start.7) | collective-permute-done | bytes 81952 | tf_op jit(solution)/shard_map/ppermute | solution.py:465
  21.5 0.4 collective-permute-done.5.refs_2_
  21.8 0.1 collective-permute-start.11
  22.0 0.4 collective-permute-start.9
  22.3 0.9 %collective-permute-done.3.refs_1_ = bf16[32,1280]{1,0:T(8,128)(2,1)S(1)} collective-permute-done((bf16[32,1280]{1,0:T(8,128)(2,1)S(1)}, bf16[32,1280]{1,0:T(8,128)(2,1)S(1)}, u32[]{:S(2)}, u32[]{:S(2)}) %collective-permute-start.3) | collective-permute-done | bytes 81952 | tf_op jit(solution)/shard_map/ppermute | solution.py:465
  23.2 3.6 %collective-permute-start.4 = (bf16[32,1280]{1,0:T(8,128)(2,1)S(1)}, bf16[32,1280]{1,0:T(8,128)(2,1)S(1)}, u32[]{:S(2)}, u32[]{:S(2)}) collective-permute-start(bf16[32,1280]{1,0:T(8,128)(2,1)S(1)} %get-tuple-element.24), channel_id=1, source_target_pairs={{0,28},{4,24},{8,20},{12,16},{16,12},{20,8},{24,4},{28,0},{1,29},{... | collective-permute-start | bytes 245768 | tf_op jit(solution)/shard_map/ppermute | solution.py:465
  26.8 0.7 %collective-permute-start = (s32[2,1,40]{2,1,0:T(1,128)S(1)}, s32[2,1,40]{2,1,0:T(1,128)S(1)}, u32[]{:S(2)}, u32[]{:S(2)}) collective-permute-start(s32[2,1,40]{2,1,0:T(1,128)S(1)} %copy-done.1), channel_id=1, source_target_pairs={{0,2},{1,3},{2,0},{3,1},{4,6},{5,7},{6,4},{7,5},{8,10},{9,11},{10,... | collective-permute-start | bytes 968 | tf_op jit(solution)/shard_map/ppermute | solution.py:460
  27.6 0.1 collective-permute-start.1
  27.7 1.3 %collective-permute-start.2 = (bf16[32,1280]{1,0:T(8,128)(2,1)S(1)}, bf16[32,1280]{1,0:T(8,128)(2,1)S(1)}, u32[]{:S(2)}, u32[]{:S(2)}) collective-permute-start(bf16[32,1280]{1,0:T(8,128)(2,1)S(1)} %get-tuple-element.22), channel_id=1, source_target_pairs={{0,24},{4,28},{8,16},{12,20},{16,8},{20,12},{24,0},{28,4},{1,25},{... | collective-permute-start | bytes 245768 | tf_op jit(solution)/shard_map/ppermute | solution.py:465
  29.0 1.4 %coefficients.5.refs_10_ = bf16[2,2,16,512]{3,2,1,0:T(8,128)(2,1)S(1)} custom-call(s32[2,1,40]{2,1,0:T(1,128)S(1)} %copy-done.1, bf16[32,1280]{1,0:T(8,128)(2,1)S(1)} %get-tuple-element.25.refs_1_, bf16[32,1280]{1,0:T(8,128)(2,1)S(1)} %collective-permute-done.5.refs_2_, bf16[32,1280]{1,0:T(8,128)(2,1)S(1)} %collective-permute-done.6.refs_3_, ...), custom_call_target="tpu_custom_call" | custom-call | flops 671088640 | bytes 1048576 | tf_op jit(solution)/shard_map/coefficients/pallas_call | solution.py:285
  30.4 0.5 collective-permute-done.4.refs_2_
  31.0 0.5 collective-permute-start.16
  31.5 1.4 %coefficients.6.refs_6_ = bf16[2,2,16,512]{3,2,1,0:T(8,128)(2,1)S(1)} custom-call(s32[2,1,40]{2,1,0:T(1,128)S(1)} %collective-permute-done.refs_0_, bf16[32,1280]{1,0:T(8,128)(2,1)S(1)} %get-tuple-element.25.refs_1_, bf16[32,1280]{1,0:T(8,128)(2,1)S(1)} %collective-permute-done.5.refs_2_, bf16[32,1280]{1,0:T(8,128)(2,1)S(1)} %collective-permute-done.6.refs_3_, ...), custom_call_target="tpu_custom_call" | custom-call | flops 671088640 | bytes 1048576 | tf_op jit(solution)/shard_map/coefficients/pallas_call | solution.py:285
  32.9 4.0 %collective-permute-done.1.refs_1_.refs_3_ = bf16[32,1280]{1,0:T(8,128)(2,1)S(1)} collective-permute-done((bf16[32,1280]{1,0:T(8,128)(2,1)S(1)}, bf16[32,1280]{1,0:T(8,128)(2,1)S(1)}, u32[]{:S(2)}, u32[]{:S(2)}) %collective-permute-start.1) | collective-permute-done | bytes 81952 | tf_op jit(solution)/shard_map/ppermute | solution.py:465
  36.9 0.5 collective-permute-start.14
  37.4 1.1 %coefficients.7.refs_6_ = bf16[2,2,16,512]{3,2,1,0:T(8,128)(2,1)S(1)} custom-call(s32[2,1,40]{2,1,0:T(1,128)S(1)} %collective-permute-done.refs_0_, bf16[32,1280]{1,0:T(8,128)(2,1)S(1)} %collective-permute-done.3.refs_1_, bf16[32,1280]{1,0:T(8,128)(2,1)S(1)} %collective-permute-done.4.refs_2_, bf16[32,1280]{1,0:T(8,128)(2,1)S(1)} %collective-permute-done.15.refs_3_.refs_5_, ...), custom_call_target="tpu_custom_call" | custom-call | flops 335544320 | bytes 1048576 | tf_op jit(solution)/shard_map/coefficients/pallas_call | solution.py:285
  38.5 1.1 %coefficients.8 = bf16[2,2,16,512]{3,2,1,0:T(8,128)(2,1)S(1)} custom-call(s32[2,1,40]{2,1,0:T(1,128)S(1)} %collective-permute-done.refs_0_, bf16[32,1280]{1,0:T(8,128)(2,1)S(1)} %collective-permute-done.1.refs_1_.refs_3_, bf16[32,1280]{1,0:T(8,128)(2,1)S(1)} %collective-permute-done.2.refs_2_.refs_4_, ...), custom_call_target="tpu_custom_call" | custom-call | flops 335544320 | bytes 1048576 | tf_op jit(solution)/shard_map/coefficients/pallas_call | solution.py:285
  39.6 0.6 %collective-permute-start.17 = (bf16[2,2,16,512]{3,2,1,0:T(8,128)(2,1)S(1)}, bf16[2,2,16,512]{3,2,1,0:T(8,128)(2,1)S(1)}, u32[]{:S(2)}, u32[]{:S(2)}) collective-permute-start(bf16[2,2,16,512]{3,2,1,0:T(8,128)(2,1)S(1)} %coefficients.8), channel_id=1, source_target_pairs={{0,2},{1,3},{2,0},{3,1},{4,6},{5,7},{6,4},{7,5},{8,10},{9,11},{10,... | collective-permute-start | bytes 196616 | tf_op jit(solution)/shard_map/ppermute | solution.py:489
  40.2 1.4 %coefficients.9.coeffs_ref = bf16[2,2,16,512]{3,2,1,0:T(8,128)(2,1)S(1)} custom-call(s32[2,1,40]{2,1,0:T(1,128)S(1)} %copy-done.1, bf16[32,1280]{1,0:T(8,128)(2,1)S(1)} %collective-permute-done.3.refs_1_, bf16[32,1280]{1,0:T(8,128)(2,1)S(1)} %collective-permute-done.4.refs_2_, bf16[32,1280]{1,0:T(8,128)(2,1)S(1)} %collective-permute-done.1.refs_1_.refs_3_, ...), custom_call_target="tpu_custom_call" | custom-call | flops 671088640 | bytes 1048576 | tf_op jit(solution)/shard_map/coefficients/pallas_call | solution.py:285
  41.7 1.0 %bands.2.refs_0_ = f32[256,128]{1,0:T(8,128)S(1)} custom-call(s32[2,1,40]{2,1,0:T(1,128)S(1)} %copy-done.1, s32[2,1,40]{2,1,0:T(1,128)S(1)} %copy-done.2, bf16[2,2,16,512]{3,2,1,0:T(8,128)(2,1)S(1)} %coefficients.9.coeffs_ref, bf16[2,2,256,512]{3,2,1,0:T(8,128)(2,1)S(1)} %bitcast.4), custom_call_target="tpu_custom_call" | custom-call | flops 134217728 | bytes 1048576 | tf_op jit(solution)/shard_map/bands/pallas_call | solution.py:357
  42.7 1.2 %collective-permute-done.17.coeffs_ref = bf16[2,2,16,512]{3,2,1,0:T(8,128)(2,1)S(1)} collective-permute-done((bf16[2,2,16,512]{3,2,1,0:T(8,128)(2,1)S(1)}, bf16[2,2,16,512]{3,2,1,0:T(8,128)(2,1)S(1)}, u32[]{:S(2)}, u32[]{:S(2)}) %collective-permute-start.17) | collective-permute-done | bytes 65568 | tf_op jit(solution)/shard_map/ppermute | solution.py:489
  44.0 1.1 %bands.3 = bf16[8,32,128]{2,1,0:T(8,128)(2,1)S(1)} custom-call(s32[2,1,40]{2,1,0:T(1,128)S(1)} %copy-done.1, s32[2,1,40]{2,1,0:T(1,128)S(1)} %copy-done.2, bf16[2,2,16,512]{3,2,1,0:T(8,128)(2,1)S(1)} %collective-permute-done.17.coeffs_ref, bf16[2,2,256,512]{3,2,1,0:T(8,128)(2,1)S(1)} %bitcast.5, f32[256,128]{1,0:T(8,128)S(1)} %bands.2.refs_0_), custom_call_target="tpu_custom_call" | custom-call | flops 134217728 | bytes 1048576 | tf_op jit(solution)/shard_map/bands/pallas_call | solution.py:357
  45.1 11.0 %all_to_all.5.bands_ref = bf16[8,32,128]{2,1,0:T(8,128)(2,1)S(1)} all-to-all(bf16[8,32,128]{2,1,0:T(8,128)(2,1)S(1)} %bands.3), channel_id=1, replica_groups=mesh['freq'=8,'rows'=4] {'freq'}, dimensions={0} | all-to-all | bytes 131072 | tf_op jit(solution)/shard_map/all_to_all | solution.py:493
  56.1 1.7 %series.1 = bf16[1024,1024]{1,0:T(8,128)(2,1)} custom-call(bf16[8,32,128]{2,1,0:T(8,128)(2,1)S(1)} %all_to_all.5.bands_ref, bf16[32,1024]{1,0:T(8,128)(2,1)S(1)} %get-tuple-element.36.table_ref), custom_call_target="tpu_custom_call" | custom-call | flops 67108864 | bytes 2097152 | tf_op jit(solution)/shard_map/series/pallas_call | solution.py:396
  (22 shorter events, 0.1 us)
Async XLA Ops:
  0.0 29.0 %copy-start.3 = (bf16[2,2,1,512,256]{4,3,2,1,0:T(8,128)(2,1)S(1)}, bf16[2,2,1,512,256]{4,3,2,1,0:T(8,128)(2,1)}, u32[]{:S(2)}) copy-start(bf16[2,2,1,512,256]{4,3,2,1,0:T(8,128)(2,1)} %param.7) | copy-start | bytes 3145732
  0.0 26.8 %copy-start.1 = (s32[2,1,40]{2,1,0:T(1,128)S(1)}, s32[2,1,40]{2,1,0:T(1,128)}, u32[]{:S(2)}) copy-start(s32[2,1,40]{2,1,0:T(1,128)} %offsets_ref.3) | copy-start | bytes 964
  0.0 41.7 %copy-start = (bf16[2,2,1,256,512]{4,3,2,1,0:T(8,128)(2,1)S(1)}, bf16[2,2,1,256,512]{4,3,2,1,0:T(8,128)(2,1)}, u32[]{:S(2)}) copy-start(bf16[2,2,1,256,512]{4,3,2,1,0:T(8,128)(2,1)} %param.6) | copy-start | bytes 3145732
  0.0 41.7 %copy-start.2 = (s32[2,1,40]{2,1,0:T(1,128)S(1)}, s32[2,1,40]{2,1,0:T(1,128)}, u32[]{:S(2)}) copy-start(s32[2,1,40]{2,1,0:T(1,128)} %ranks_ref.3) | copy-start | bytes 964
  0.0 31.5 %collective-permute-start.12 = (bf16[2,2,512,256]{3,2,1,0:T(8,128)(2,1)}, bf16[2,2,512,256]{3,2,1,0:T(8,128)(2,1)S(1)}, u32[]{:S(2)}, u32[]{:S(2)}) collective-permute-start(bf16[2,2,512,256]{3,2,1,0:T(8,128)(2,1)} %bitcast.6), channel_id=1, source_target_pairs={{0,2},{1,3},{2,0},{3,1},{4,6},{5,7},{6,4},{7,5},{8,10},{9,11},{10,... | collective-permute-start | bytes 3145736 | tf_op jit(solution)/shard_map/ppermute | solution.py:459
  12.7 5.6 %collective-permute-start.6 = (bf16[32,1280]{1,0:T(8,128)(2,1)S(1)}, bf16[32,1280]{1,0:T(8,128)(2,1)S(1)}, u32[]{:S(2)}, u32[]{:S(2)}) collective-permute-start(bf16[32,1280]{1,0:T(8,128)(2,1)S(1)} %get-tuple-element.27), channel_id=1, source_target_pairs={{0,8},{4,12},{8,0},{12,4},{16,24},{20,28},{24,16},{28,20},{1,9},{5... | collective-permute-start | bytes 245768 | tf_op jit(solution)/shard_map/ppermute | solution.py:465
  14.3 7.2 %collective-permute-start.7 = (bf16[32,1280]{1,0:T(8,128)(2,1)S(1)}, bf16[32,1280]{1,0:T(8,128)(2,1)S(1)}, u32[]{:S(2)}, u32[]{:S(2)}) collective-permute-start(bf16[32,1280]{1,0:T(8,128)(2,1)S(1)} %get-tuple-element.28), channel_id=1, source_target_pairs={{0,12},{4,8},{8,4},{12,0},{16,28},{20,24},{24,20},{28,16},{1,13},{... | collective-permute-start | bytes 245768 | tf_op jit(solution)/shard_map/ppermute | solution.py:465
  15.7 6.1 %collective-permute-start.5 = (bf16[32,1280]{1,0:T(8,128)(2,1)S(1)}, bf16[32,1280]{1,0:T(8,128)(2,1)S(1)}, u32[]{:S(2)}, u32[]{:S(2)}) collective-permute-start(bf16[32,1280]{1,0:T(8,128)(2,1)S(1)} %get-tuple-element.26), channel_id=1, source_target_pairs={{0,16},{4,20},{8,24},{12,28},{16,0},{20,4},{24,8},{28,12},{1,17},{... | collective-permute-start | bytes 245768 | tf_op jit(solution)/shard_map/ppermute | solution.py:465
  18.3 3.7 %collective-permute-start.8 = (bf16[32,1280]{1,0:T(8,128)(2,1)S(1)}, bf16[32,1280]{1,0:T(8,128)(2,1)S(1)}, u32[]{:S(2)}, u32[]{:S(2)}) collective-permute-start(bf16[32,1280]{1,0:T(8,128)(2,1)S(1)} %get-tuple-element.25.refs_1_), channel_id=1, source_target_pairs={{0,1},{1,0},{2,3},{3,2},{4,5},{5,4},{6,7},{7,6},{8,9},{9,8},{10,11... | collective-permute-start | bytes 245768 | tf_op jit(solution)/shard_map/ppermute | solution.py:471
  18.3 4.9 %collective-permute-start.3 = (bf16[32,1280]{1,0:T(8,128)(2,1)S(1)}, bf16[32,1280]{1,0:T(8,128)(2,1)S(1)}, u32[]{:S(2)}, u32[]{:S(2)}) collective-permute-start(bf16[32,1280]{1,0:T(8,128)(2,1)S(1)} %get-tuple-element.23), channel_id=1, source_target_pairs={{0,4},{4,0},{8,12},{12,8},{16,20},{20,16},{24,28},{28,24},{1,5},{5... | collective-permute-start | bytes 245768 | tf_op jit(solution)/shard_map/ppermute | solution.py:465
  21.5 5.4 %collective-permute-start.10 = (bf16[32,1280]{1,0:T(8,128)(2,1)S(1)}, bf16[32,1280]{1,0:T(8,128)(2,1)S(1)}, u32[]{:S(2)}, u32[]{:S(2)}) collective-permute-start(bf16[32,1280]{1,0:T(8,128)(2,1)S(1)} %collective-permute-done.6.refs_3_), channel_id=1, source_target_pairs={{0,1},{1,0},{2,3},{3,2},{4,5},{5,4},{6,7},{7,6},{8,9},{9,8},{10,11... | collective-permute-start | bytes 245768 | tf_op jit(solution)/shard_map/ppermute | solution.py:471
  21.8 5.7 %collective-permute-start.11 = (bf16[32,1280]{1,0:T(8,128)(2,1)S(1)}, bf16[32,1280]{1,0:T(8,128)(2,1)S(1)}, u32[]{:S(2)}, u32[]{:S(2)}) collective-permute-start(bf16[32,1280]{1,0:T(8,128)(2,1)S(1)} %collective-permute-done.7.refs_4_), channel_id=1, source_target_pairs={{0,1},{1,0},{2,3},{3,2},{4,5},{5,4},{6,7},{7,6},{8,9},{9,8},{10,11... | collective-permute-start | bytes 245768 | tf_op jit(solution)/shard_map/ppermute | solution.py:471
  22.0 5.7 %collective-permute-start.9 = (bf16[32,1280]{1,0:T(8,128)(2,1)S(1)}, bf16[32,1280]{1,0:T(8,128)(2,1)S(1)}, u32[]{:S(2)}, u32[]{:S(2)}) collective-permute-start(bf16[32,1280]{1,0:T(8,128)(2,1)S(1)} %collective-permute-done.5.refs_2_), channel_id=1, source_target_pairs={{0,1},{1,0},{2,3},{3,2},{4,5},{5,4},{6,7},{7,6},{8,9},{9,8},{10,11... | collective-permute-start | bytes 245768 | tf_op jit(solution)/shard_map/ppermute | solution.py:471
  23.2 7.7 %collective-permute-start.4 = (bf16[32,1280]{1,0:T(8,128)(2,1)S(1)}, bf16[32,1280]{1,0:T(8,128)(2,1)S(1)}, u32[]{:S(2)}, u32[]{:S(2)}) collective-permute-start(bf16[32,1280]{1,0:T(8,128)(2,1)S(1)} %get-tuple-element.24), channel_id=1, source_target_pairs={{0,28},{4,24},{8,20},{12,16},{16,12},{20,8},{24,4},{28,0},{1,29},{... | collective-permute-start | bytes 245768 | tf_op jit(solution)/shard_map/ppermute | solution.py:465
  26.8 4.1 %collective-permute-start = (s32[2,1,40]{2,1,0:T(1,128)S(1)}, s32[2,1,40]{2,1,0:T(1,128)S(1)}, u32[]{:S(2)}, u32[]{:S(2)}) collective-permute-start(s32[2,1,40]{2,1,0:T(1,128)S(1)} %copy-done.1), channel_id=1, source_target_pairs={{0,2},{1,3},{2,0},{3,1},{4,6},{5,7},{6,4},{7,5},{8,10},{9,11},{10,... | collective-permute-start | bytes 968 | tf_op jit(solution)/shard_map/ppermute | solution.py:460
  27.6 9.3 %collective-permute-start.1 = (bf16[32,1280]{1,0:T(8,128)(2,1)S(1)}, bf16[32,1280]{1,0:T(8,128)(2,1)S(1)}, u32[]{:S(2)}, u32[]{:S(2)}) collective-permute-start(bf16[32,1280]{1,0:T(8,128)(2,1)S(1)} %get-tuple-element.21), channel_id=1, source_target_pairs={{0,20},{4,16},{8,28},{12,24},{16,4},{20,0},{24,12},{28,8},{1,21},{... | collective-permute-start | bytes 245768 | tf_op jit(solution)/shard_map/ppermute | solution.py:465
  27.7 9.2 %collective-permute-start.2 = (bf16[32,1280]{1,0:T(8,128)(2,1)S(1)}, bf16[32,1280]{1,0:T(8,128)(2,1)S(1)}, u32[]{:S(2)}, u32[]{:S(2)}) collective-permute-start(bf16[32,1280]{1,0:T(8,128)(2,1)S(1)} %get-tuple-element.22), channel_id=1, source_target_pairs={{0,24},{4,28},{8,16},{12,20},{16,8},{20,12},{24,0},{28,4},{1,25},{... | collective-permute-start | bytes 245768 | tf_op jit(solution)/shard_map/ppermute | solution.py:465
  30.9 6.5 %collective-permute-start.15 = (bf16[32,1280]{1,0:T(8,128)(2,1)S(1)}, bf16[32,1280]{1,0:T(8,128)(2,1)S(1)}, u32[]{:S(2)}, u32[]{:S(2)}) collective-permute-start(bf16[32,1280]{1,0:T(8,128)(2,1)S(1)} %collective-permute-done.3.refs_1_), channel_id=1, source_target_pairs={{0,1},{1,0},{2,3},{3,2},{4,5},{5,4},{6,7},{7,6},{8,9},{9,8},{10,11... | collective-permute-start | bytes 245768 | tf_op jit(solution)/shard_map/ppermute | solution.py:471
  31.0 6.5 %collective-permute-start.16 = (bf16[32,1280]{1,0:T(8,128)(2,1)S(1)}, bf16[32,1280]{1,0:T(8,128)(2,1)S(1)}, u32[]{:S(2)}, u32[]{:S(2)}) collective-permute-start(bf16[32,1280]{1,0:T(8,128)(2,1)S(1)} %collective-permute-done.4.refs_2_), channel_id=1, source_target_pairs={{0,1},{1,0},{2,3},{3,2},{4,5},{5,4},{6,7},{7,6},{8,9},{9,8},{10,11... | collective-permute-start | bytes 245768 | tf_op jit(solution)/shard_map/ppermute | solution.py:471
  36.9 1.6 %collective-permute-start.13 = (bf16[32,1280]{1,0:T(8,128)(2,1)S(1)}, bf16[32,1280]{1,0:T(8,128)(2,1)S(1)}, u32[]{:S(2)}, u32[]{:S(2)}) collective-permute-start(bf16[32,1280]{1,0:T(8,128)(2,1)S(1)} %collective-permute-done.1.refs_1_.refs_3_), channel_id=1, source_target_pairs={{0,1},{1,0},{2,3},{3,2},{4,5},{5,4},{6,7},{7,6},{8,9},{9,8},{10,11... | collective-permute-start | bytes 245768 | tf_op jit(solution)/shard_map/ppermute | solution.py:471
  36.9 1.6 %collective-permute-start.14 = (bf16[32,1280]{1,0:T(8,128)(2,1)S(1)}, bf16[32,1280]{1,0:T(8,128)(2,1)S(1)}, u32[]{:S(2)}, u32[]{:S(2)}) collective-permute-start(bf16[32,1280]{1,0:T(8,128)(2,1)S(1)} %collective-permute-done.2.refs_2_.refs_4_), channel_id=1, source_target_pairs={{0,1},{1,0},{2,3},{3,2},{4,5},{5,4},{6,7},{7,6},{8,9},{9,8},{10,11... | collective-permute-start | bytes 245768 | tf_op jit(solution)/shard_map/ppermute | solution.py:471
  39.6 4.3 %collective-permute-start.17 = (bf16[2,2,16,512]{3,2,1,0:T(8,128)(2,1)S(1)}, bf16[2,2,16,512]{3,2,1,0:T(8,128)(2,1)S(1)}, u32[]{:S(2)}, u32[]{:S(2)}) collective-permute-start(bf16[2,2,16,512]{3,2,1,0:T(8,128)(2,1)S(1)} %coefficients.8), channel_id=1, source_target_pairs={{0,2},{1,3},{2,0},{3,1},{4,6},{5,7},{6,4},{7,5},{8,10},{9,11},{10,... | collective-permute-start | bytes 196616 | tf_op jit(solution)/shard_map/ppermute | solution.py:489
where the time goes:
time: 58 us; the launch traced here: 57.8 us
  Pallas kernels  19.9 us (34%)
  starting transfers between devices  18.5 us (32%)
  blocking collectives  11 us (19%)
  waiting for transfers between devices  8.19 us (14%)
    ppermute x7, starting transfers between devices, per_device_fast(): own[shift] = lax.ppermute(sent[shift], 'freq', swap)  12.6 us
    all_to_all x1, blocking collectives, per_device_fast(): lax.all_to_all(bands, 'freq', split_axis=0, concat_axis=0, tiled=True)  11 us
    pallas_call x1, Pallas kernels, transform(): pl.pallas_call(transform_kernel, in_specs=[pl.BlockSpec(memory_space=pltp...  9.61 us
    ppermute x7, waiting for transfers between devices, per_device_fast(): own[shift] = lax.ppermute(sent[shift], 'freq', swap)  6.92 us
    pallas_call x5, Pallas kernels, coefficients(): pl.pallas_call(functools.partial(coefficient_kernel, tuple(shifts), sides...  6.51 us
    ppermute x1, starting transfers between devices, per_device_fast(): v_far = lax.ppermute(v_own, 'rows', across)  3.04 us
    pallas_call x2, Pallas kernels, bands_of(): pl.pallas_call(functools.partial(band_kernel, add, at_near), in_specs=[SM...  2.13 us
    pallas_call x1, Pallas kernels, series_of(): pl.pallas_call(functools.partial(series_kernel, scale), in_specs=[VMEM] *...  1.66 us
  transfers between devices with their start and end apart: 18, of which 6 were waited for; matrix products, arithmetic and copies ran while one was open for 0% of the time, Pallas kernels for 28%

commit v1 on v0

--- a/solution.py
+++ b/solution.py
@@ -440,9 +440,10 @@
 
 def arrivals(groups):
     order = shift_order(groups)
-    crossing = [s for s in order[1:] if s >= groups // 2]
-    early = [s for s in order if s not in crossing and s != 1]
-    return [0] + early, [1] + crossing[:-2], crossing[-2:]
+    last = [s for s in order[1:] if s >= groups // 2][-2:]
+    early = [s for s in order[:2] if s not in last]
+    middle = sorted((s for s in order if s not in early + last), key=lambda s: s >= groups // 2)
+    return [0] + early, middle, last
 
 
 def per_device_fast(wavefield, u_factors, v_factors, tile_ranks, tile_offsets):

time: 58 us -> 56.6 us (0.976)
  starting transfers between devices: 18.5 us -> 17.2 us
  blocking collectives: 11 us -> 10.2 us
  waiting for transfers between devices: 8.19 us -> 8.99 us
    ppermute x7, starting transfers between devices: 12.6 us -> 11.4 us  [per_device_fast(): own[shift] = lax.ppermute(sent[shift], 'freq', swap)]
    ppermute x7, waiting for transfers between devices: 6.92 us -> 7.8 us  [per_device_fast(): own[shift] = lax.ppermute(sent[shift], 'freq', swap)]
    all_to_all x1, blocking collectives: 11 us -> 10.2 us  [per_device_fast(): lax.all_to_all(bands, 'freq', split_axis=0, concat_axis=0, tiled=True)]
  transfers between devices with their start and end apart: 18 -> 18, of which waited for: 6 -> 5; matrix products, arithmetic and copies ran while one was open for 0% -> 0% of each run, Pallas kernels for 28% -> 28%
where the time goes in v1:
time: 56.6 us; the launch traced here: 56.4 us
  Pallas kernels  19.9 us (35%)
  starting transfers between devices  17.2 us (30%)
  blocking collectives  10.2 us (18%)
  waiting for transfers between devices  8.99 us (16%)
    ppermute x7, starting transfers between devices, per_device_fast(): own[shift] = lax.ppermute(sent[shift], 'freq', swap)  11.4 us
    all_to_all x1, blocking collectives, per_device_fast(): lax.all_to_all(bands, 'freq', split_axis=0, concat_axis=0, tiled=True)  10.2 us
    pallas_call x1, Pallas kernels, transform(): pl.pallas_call(transform_kernel, in_specs=[pl.BlockSpec(memory_space=pltp...  9.61 us
    ppermute x7, waiting for transfers between devices, per_device_fast(): own[shift] = lax.ppermute(sent[shift], 'freq', swap)  7.8 us
    pallas_call x5, Pallas kernels, coefficients(): pl.pallas_call(functools.partial(coefficient_kernel, tuple(shifts), sides...  6.51 us
    ppermute x1, starting transfers between devices, per_device_fast(): v_far = lax.ppermute(v_own, 'rows', across)  3.04 us
    pallas_call x2, Pallas kernels, bands_of(): pl.pallas_call(functools.partial(band_kernel, add, at_near), in_specs=[SM...  2.13 us
    pallas_call x1, Pallas kernels, series_of(): pl.pallas_call(functools.partial(series_kernel, scale), in_specs=[VMEM] *...  1.66 us
  transfers between devices with their start and end apart: 18, of which 5 were waited for; matrix products, arithmetic and copies ran while one was open for 0% of the time, Pallas kernels for 28%

profile of v1, /device:TPU:0, one launch (start us, length us, event | category | flops | bytes accessed | tf_op | source)
XLA Modules:
  0.0 56.4 jit_solution(16719587576077880654)
XLA Ops:
  0.0 3.0 %collective-permute-start.11 = (bf16[2,2,512,256]{3,2,1,0:T(8,128)(2,1)}, bf16[2,2,512,256]{3,2,1,0:T(8,128)(2,1)S(1)}, u32[]{:S(2)}, u32[]{:S(2)}) collective-permute-start(bf16[2,2,512,256]{3,2,1,0:T(8,128)(2,1)} %bitcast.6), channel_id=1, source_target_pairs={{0,2},{1,3},{2,0},{3,1},{4,6},{5,7},{6,4},{7,5},{8,10},{9,11},{10,... | collective-permute-start | bytes 3145736 | tf_op jit(solution)/shard_map/ppermute | solution.py:460
  3.1 9.6 %transform.1 = (bf16[32,1280]{1,0:T(8,128)(2,1)S(1)}, bf16[32,1280]{1,0:T(8,128)(2,1)S(1)}, bf16[32,1280]{1,0:T(8,128)(2,1)S(1)}, bf16[32,1280]{1,0:T(8,128)(2,1...) custom-call(bf16[10240,1024]{1,0:T(8,128)(2,1)} %bitcast.9), custom_call_target="tpu_custom_call" | custom-call | flops 5368709120 | bytes 20971520 | tf_op jit(solution)/shard_map/transform/pallas_call | solution.py:194
  12.7 1.6 %collective-permute-start.7 = (bf16[32,1280]{1,0:T(8,128)(2,1)S(1)}, bf16[32,1280]{1,0:T(8,128)(2,1)S(1)}, u32[]{:S(2)}, u32[]{:S(2)}) collective-permute-start(bf16[32,1280]{1,0:T(8,128)(2,1)S(1)} %get-tuple-element.29), channel_id=1, source_target_pairs={{0,8},{4,12},{8,0},{12,4},{16,24},{20,28},{24,16},{28,20},{1,9},{5... | collective-permute-start | bytes 245768 | tf_op jit(solution)/shard_map/ppermute | solution.py:466
  14.3 2.6 %collective-permute-start.6 = (bf16[32,1280]{1,0:T(8,128)(2,1)S(1)}, bf16[32,1280]{1,0:T(8,128)(2,1)S(1)}, u32[]{:S(2)}, u32[]{:S(2)}) collective-permute-start(bf16[32,1280]{1,0:T(8,128)(2,1)S(1)} %get-tuple-element.28), channel_id=1, source_target_pairs={{0,16},{4,20},{8,24},{12,28},{16,0},{20,4},{24,8},{28,12},{1,17},{... | collective-permute-start | bytes 245768 | tf_op jit(solution)/shard_map/ppermute | solution.py:466
  16.9 0.0 collective-permute-start.8
  16.9 1.4 %collective-permute-start.3 = (bf16[32,1280]{1,0:T(8,128)(2,1)S(1)}, bf16[32,1280]{1,0:T(8,128)(2,1)S(1)}, u32[]{:S(2)}, u32[]{:S(2)}) collective-permute-start(bf16[32,1280]{1,0:T(8,128)(2,1)S(1)} %get-tuple-element.24), channel_id=1, source_target_pairs={{0,12},{4,8},{8,4},{12,0},{16,28},{20,24},{24,20},{28,16},{1,13},{... | collective-permute-start | bytes 245768 | tf_op jit(solution)/shard_map/ppermute | solution.py:466
  18.3 0.0 collective-permute-done.7.refs_3_
  18.3 0.5 collective-permute-start.4
  18.8 1.8 %collective-permute-done.6.refs_2_ = bf16[32,1280]{1,0:T(8,128)(2,1)S(1)} collective-permute-done((bf16[32,1280]{1,0:T(8,128)(2,1)S(1)}, bf16[32,1280]{1,0:T(8,128)(2,1)S(1)}, u32[]{:S(2)}, u32[]{:S(2)}) %collective-permute-start.6) | collective-permute-done | bytes 81952 | tf_op jit(solution)/shard_map/ppermute | solution.py:466
  20.6 0.5 collective-permute-start.9
  21.2 1.7 %collective-permute-done.3.refs_1_ = bf16[32,1280]{1,0:T(8,128)(2,1)S(1)} collective-permute-done((bf16[32,1280]{1,0:T(8,128)(2,1)S(1)}, bf16[32,1280]{1,0:T(8,128)(2,1)S(1)}, u32[]{:S(2)}, u32[]{:S(2)}) %collective-permute-start.3) | collective-permute-done | bytes 81952 | tf_op jit(solution)/shard_map/ppermute | solution.py:466
  22.9 2.1 %collective-permute-start.5 = (bf16[32,1280]{1,0:T(8,128)(2,1)S(1)}, bf16[32,1280]{1,0:T(8,128)(2,1)S(1)}, u32[]{:S(2)}, u32[]{:S(2)}) collective-permute-start(bf16[32,1280]{1,0:T(8,128)(2,1)S(1)} %get-tuple-element.26), channel_id=1, source_target_pairs={{0,28},{4,24},{8,20},{12,16},{16,12},{20,8},{24,4},{28,0},{1,29},{... | collective-permute-start | bytes 245768 | tf_op jit(solution)/shard_map/ppermute | solution.py:466
  24.9 0.0 collective-permute-done.4.refs_2_
  24.9 0.6 %collective-permute-start = (s32[2,1,40]{2,1,0:T(1,128)S(1)}, s32[2,1,40]{2,1,0:T(1,128)S(1)}, u32[]{:S(2)}, u32[]{:S(2)}) collective-permute-start(s32[2,1,40]{2,1,0:T(1,128)S(1)} %copy-done.1), channel_id=1, source_target_pairs={{0,2},{1,3},{2,0},{3,1},{4,6},{5,7},{6,4},{7,5},{8,10},{9,11},{10,... | collective-permute-start | bytes 968 | tf_op jit(solution)/shard_map/ppermute | solution.py:461
  25.6 1.5 %collective-permute-start.1 = (bf16[32,1280]{1,0:T(8,128)(2,1)S(1)}, bf16[32,1280]{1,0:T(8,128)(2,1)S(1)}, u32[]{:S(2)}, u32[]{:S(2)}) collective-permute-start(bf16[32,1280]{1,0:T(8,128)(2,1)S(1)} %get-tuple-element.22), channel_id=1, source_target_pairs={{0,20},{4,16},{8,28},{12,24},{16,4},{20,0},{24,12},{28,8},{1,21},{... | collective-permute-start | bytes 245768 | tf_op jit(solution)/shard_map/ppermute | solution.py:466
  27.1 1.7 %collective-permute-start.2 = (bf16[32,1280]{1,0:T(8,128)(2,1)S(1)}, bf16[32,1280]{1,0:T(8,128)(2,1)S(1)}, u32[]{:S(2)}, u32[]{:S(2)}) collective-permute-start(bf16[32,1280]{1,0:T(8,128)(2,1)S(1)} %get-tuple-element.23), channel_id=1, source_target_pairs={{0,24},{4,28},{8,16},{12,20},{16,8},{20,12},{24,0},{28,4},{1,25},{... | collective-permute-start | bytes 245768 | tf_op jit(solution)/shard_map/ppermute | solution.py:466
  28.8 1.3 %coefficients.5.refs_12_ = bf16[2,2,16,512]{3,2,1,0:T(8,128)(2,1)S(1)} custom-call(s32[2,1,40]{2,1,0:T(1,128)S(1)} %copy-done.1, bf16[32,1280]{1,0:T(8,128)(2,1)S(1)} %get-tuple-element.27.refs_1_, bf16[32,1280]{1,0:T(8,128)(2,1)S(1)} %collective-permute-done.6.refs_2_, bf16[32,1280]{1,0:T(8,128)(2,1)S(1)} %collective-permute-done.7.refs_3_, ...), custom_call_target="tpu_custom_call" | custom-call | flops 503316480 | bytes 1048576 | tf_op jit(solution)/shard_map/coefficients/pallas_call | solution.py:285
  30.0 0.5 collective-permute-done.5.refs_3_
  30.6 0.5 collective-permute-start.15
  31.1 0.1 collective-permute-start.16
  31.2 1.3 %coefficients.6.refs_8_ = bf16[2,2,16,512]{3,2,1,0:T(8,128)(2,1)S(1)} custom-call(s32[2,1,40]{2,1,0:T(1,128)S(1)} %collective-permute-done.refs_0_, bf16[32,1280]{1,0:T(8,128)(2,1)S(1)} %get-tuple-element.27.refs_1_, bf16[32,1280]{1,0:T(8,128)(2,1)S(1)} %collective-permute-done.6.refs_2_, bf16[32,1280]{1,0:T(8,128)(2,1)S(1)} %collective-permute-done.7.refs_3_, ...), custom_call_target="tpu_custom_call" | custom-call | flops 503316480 | bytes 1048576 | tf_op jit(solution)/shard_map/coefficients/pallas_call | solution.py:285
  32.4 3.7 %collective-permute-done.1.refs_1_.refs_4_ = bf16[32,1280]{1,0:T(8,128)(2,1)S(1)} collective-permute-done((bf16[32,1280]{1,0:T(8,128)(2,1)S(1)}, bf16[32,1280]{1,0:T(8,128)(2,1)S(1)}, u32[]{:S(2)}, u32[]{:S(2)}) %collective-permute-start.1) | collective-permute-done | bytes 81952 | tf_op jit(solution)/shard_map/ppermute | solution.py:466
  36.2 0.5 collective-permute-start.13
  36.7 1.3 %coefficients.7.refs_6_ = bf16[2,2,16,512]{3,2,1,0:T(8,128)(2,1)S(1)} custom-call(s32[2,1,40]{2,1,0:T(1,128)S(1)} %collective-permute-done.refs_0_, bf16[32,1280]{1,0:T(8,128)(2,1)S(1)} %collective-permute-done.3.refs_1_, bf16[32,1280]{1,0:T(8,128)(2,1)S(1)} %collective-permute-done.4.refs_2_, bf16[32,1280]{1,0:T(8,128)(2,1)S(1)} %collective-permute-done.5.refs_3_, ...), custom_call_target="tpu_custom_call" | custom-call | flops 503316480 | bytes 1048576 | tf_op jit(solution)/shard_map/coefficients/pallas_call | solution.py:285
  38.0 1.1 %coefficients.8 = bf16[2,2,16,512]{3,2,1,0:T(8,128)(2,1)S(1)} custom-call(s32[2,1,40]{2,1,0:T(1,128)S(1)} %collective-permute-done.refs_0_, bf16[32,1280]{1,0:T(8,128)(2,1)S(1)} %collective-permute-done.1.refs_1_.refs_4_, bf16[32,1280]{1,0:T(8,128)(2,1)S(1)} %collective-permute-done.2.refs_2_.refs_5_, ...), custom_call_target="tpu_custom_call" | custom-call | flops 335544320 | bytes 1048576 | tf_op jit(solution)/shard_map/coefficients/pallas_call | solution.py:285
  39.1 0.5 collective-permute-start.17
  39.6 1.6 %coefficients.9.coeffs_ref = bf16[2,2,16,512]{3,2,1,0:T(8,128)(2,1)S(1)} custom-call(s32[2,1,40]{2,1,0:T(1,128)S(1)} %copy-done.1, bf16[32,1280]{1,0:T(8,128)(2,1)S(1)} %collective-permute-done.3.refs_1_, bf16[32,1280]{1,0:T(8,128)(2,1)S(1)} %collective-permute-done.4.refs_2_, bf16[32,1280]{1,0:T(8,128)(2,1)S(1)} %collective-permute-done.5.refs_3_, ...), custom_call_target="tpu_custom_call" | custom-call | flops 838860800 | bytes 1048576 | tf_op jit(solution)/shard_map/coefficients/pallas_call | solution.py:285
  41.2 1.0 %bands.2.refs_0_ = f32[256,128]{1,0:T(8,128)S(1)} custom-call(s32[2,1,40]{2,1,0:T(1,128)S(1)} %copy-done.1, s32[2,1,40]{2,1,0:T(1,128)S(1)} %copy-done.2, bf16[2,2,16,512]{3,2,1,0:T(8,128)(2,1)S(1)} %coefficients.9.coeffs_ref, bf16[2,2,256,512]{3,2,1,0:T(8,128)(2,1)S(1)} %bitcast.4), custom_call_target="tpu_custom_call" | custom-call | flops 134217728 | bytes 1048576 | tf_op jit(solution)/shard_map/bands/pallas_call | solution.py:357
  42.3 1.2 %collective-permute-done.17.coeffs_ref = bf16[2,2,16,512]{3,2,1,0:T(8,128)(2,1)S(1)} collective-permute-done((bf16[2,2,16,512]{3,2,1,0:T(8,128)(2,1)S(1)}, bf16[2,2,16,512]{3,2,1,0:T(8,128)(2,1)S(1)}, u32[]{:S(2)}, u32[]{:S(2)}) %collective-permute-start.17) | collective-permute-done | bytes 65568 | tf_op jit(solution)/shard_map/ppermute | solution.py:490
  43.4 1.1 %bands.3 = bf16[8,32,128]{2,1,0:T(8,128)(2,1)S(1)} custom-call(s32[2,1,40]{2,1,0:T(1,128)S(1)} %copy-done.1, s32[2,1,40]{2,1,0:T(1,128)S(1)} %copy-done.2, bf16[2,2,16,512]{3,2,1,0:T(8,128)(2,1)S(1)} %collective-permute-done.17.coeffs_ref, bf16[2,2,256,512]{3,2,1,0:T(8,128)(2,1)S(1)} %bitcast.5, f32[256,128]{1,0:T(8,128)S(1)} %bands.2.refs_0_), custom_call_target="tpu_custom_call" | custom-call | flops 134217728 | bytes 1048576 | tf_op jit(solution)/shard_map/bands/pallas_call | solution.py:357
  44.5 10.2 %all_to_all.5.bands_ref = bf16[8,32,128]{2,1,0:T(8,128)(2,1)S(1)} all-to-all(bf16[8,32,128]{2,1,0:T(8,128)(2,1)S(1)} %bands.3), channel_id=1, replica_groups=mesh['freq'=8,'rows'=4] {'freq'}, dimensions={0} | all-to-all | bytes 131072 | tf_op jit(solution)/shard_map/all_to_all | solution.py:494
  54.8 1.7 %series.1 = bf16[1024,1024]{1,0:T(8,128)(2,1)} custom-call(bf16[8,32,128]{2,1,0:T(8,128)(2,1)S(1)} %all_to_all.5.bands_ref, bf16[32,1024]{1,0:T(8,128)(2,1)S(1)} %get-tuple-element.38.table_ref), custom_call_target="tpu_custom_call" | custom-call | flops 67108864 | bytes 2097152 | tf_op jit(solution)/shard_map/series/pallas_call | solution.py:396
  (22 shorter events, 0.1 us)
Async XLA Ops:
  0.0 28.8 %copy-start.3 = (bf16[2,2,1,512,256]{4,3,2,1,0:T(8,128)(2,1)S(1)}, bf16[2,2,1,512,256]{4,3,2,1,0:T(8,128)(2,1)}, u32[]{:S(2)}) copy-start(bf16[2,2,1,512,256]{4,3,2,1,0:T(8,128)(2,1)} %param.7) | copy-start | bytes 3145732
  0.0 24.9 %copy-start.1 = (s32[2,1,40]{2,1,0:T(1,128)S(1)}, s32[2,1,40]{2,1,0:T(1,128)}, u32[]{:S(2)}) copy-start(s32[2,1,40]{2,1,0:T(1,128)} %offsets_ref.3) | copy-start | bytes 964
  0.0 41.2 %copy-start = (bf16[2,2,1,256,512]{4,3,2,1,0:T(8,128)(2,1)S(1)}, bf16[2,2,1,256,512]{4,3,2,1,0:T(8,128)(2,1)}, u32[]{:S(2)}) copy-start(bf16[2,2,1,256,512]{4,3,2,1,0:T(8,128)(2,1)} %param.6) | copy-start | bytes 3145732
  0.0 41.2 %copy-start.2 = (s32[2,1,40]{2,1,0:T(1,128)S(1)}, s32[2,1,40]{2,1,0:T(1,128)}, u32[]{:S(2)}) copy-start(s32[2,1,40]{2,1,0:T(1,128)} %ranks_ref.3) | copy-start | bytes 964
  0.0 31.1 %collective-permute-start.11 = (bf16[2,2,512,256]{3,2,1,0:T(8,128)(2,1)}, bf16[2,2,512,256]{3,2,1,0:T(8,128)(2,1)S(1)}, u32[]{:S(2)}, u32[]{:S(2)}) collective-permute-start(bf16[2,2,512,256]{3,2,1,0:T(8,128)(2,1)} %bitcast.6), channel_id=1, source_target_pairs={{0,2},{1,3},{2,0},{3,1},{4,6},{5,7},{6,4},{7,5},{8,10},{9,11},{10,... | collective-permute-start | bytes 3145736 | tf_op jit(solution)/shard_map/ppermute | solution.py:460
  12.7 5.6 %collective-permute-start.7 = (bf16[32,1280]{1,0:T(8,128)(2,1)S(1)}, bf16[32,1280]{1,0:T(8,128)(2,1)S(1)}, u32[]{:S(2)}, u32[]{:S(2)}) collective-permute-start(bf16[32,1280]{1,0:T(8,128)(2,1)S(1)} %get-tuple-element.29), channel_id=1, source_target_pairs={{0,8},{4,12},{8,0},{12,4},{16,24},{20,28},{24,16},{28,20},{1,9},{5... | collective-permute-start | bytes 245768 | tf_op jit(solution)/shard_map/ppermute | solution.py:466
  14.3 6.3 %collective-permute-start.6 = (bf16[32,1280]{1,0:T(8,128)(2,1)S(1)}, bf16[32,1280]{1,0:T(8,128)(2,1)S(1)}, u32[]{:S(2)}, u32[]{:S(2)}) collective-permute-start(bf16[32,1280]{1,0:T(8,128)(2,1)S(1)} %get-tuple-element.28), channel_id=1, source_target_pairs={{0,16},{4,20},{8,24},{12,28},{16,0},{20,4},{24,8},{28,12},{1,17},{... | collective-permute-start | bytes 245768 | tf_op jit(solution)/shard_map/ppermute | solution.py:466
  16.9 3.8 %collective-permute-start.8 = (bf16[32,1280]{1,0:T(8,128)(2,1)S(1)}, bf16[32,1280]{1,0:T(8,128)(2,1)S(1)}, u32[]{:S(2)}, u32[]{:S(2)}) collective-permute-start(bf16[32,1280]{1,0:T(8,128)(2,1)S(1)} %get-tuple-element.27.refs_1_), channel_id=1, source_target_pairs={{0,1},{1,0},{2,3},{3,2},{4,5},{5,4},{6,7},{7,6},{8,9},{9,8},{10,11... | collective-permute-start | bytes 245768 | tf_op jit(solution)/shard_map/ppermute | solution.py:472
  16.9 6.0 %collective-permute-start.3 = (bf16[32,1280]{1,0:T(8,128)(2,1)S(1)}, bf16[32,1280]{1,0:T(8,128)(2,1)S(1)}, u32[]{:S(2)}, u32[]{:S(2)}) collective-permute-start(bf16[32,1280]{1,0:T(8,128)(2,1)S(1)} %get-tuple-element.24), channel_id=1, source_target_pairs={{0,12},{4,8},{8,4},{12,0},{16,28},{20,24},{24,20},{28,16},{1,13},{... | collective-permute-start | bytes 245768 | tf_op jit(solution)/shard_map/ppermute | solution.py:466
  18.3 6.6 %collective-permute-start.4 = (bf16[32,1280]{1,0:T(8,128)(2,1)S(1)}, bf16[32,1280]{1,0:T(8,128)(2,1)S(1)}, u32[]{:S(2)}, u32[]{:S(2)}) collective-permute-start(bf16[32,1280]{1,0:T(8,128)(2,1)S(1)} %get-tuple-element.25), channel_id=1, source_target_pairs={{0,4},{4,0},{8,12},{12,8},{16,20},{20,16},{24,28},{28,24},{1,5},{5... | collective-permute-start | bytes 245768 | tf_op jit(solution)/shard_map/ppermute | solution.py:466
  20.6 4.9 %collective-permute-start.10 = (bf16[32,1280]{1,0:T(8,128)(2,1)S(1)}, bf16[32,1280]{1,0:T(8,128)(2,1)S(1)}, u32[]{:S(2)}, u32[]{:S(2)}) collective-permute-start(bf16[32,1280]{1,0:T(8,128)(2,1)S(1)} %collective-permute-done.7.refs_3_), channel_id=1, source_target_pairs={{0,1},{1,0},{2,3},{3,2},{4,5},{5,4},{6,7},{7,6},{8,9},{9,8},{10,11... | collective-permute-start | bytes 245768 | tf_op jit(solution)/shard_map/ppermute | solution.py:472
  20.6 6.5 %collective-permute-start.9 = (bf16[32,1280]{1,0:T(8,128)(2,1)S(1)}, bf16[32,1280]{1,0:T(8,128)(2,1)S(1)}, u32[]{:S(2)}, u32[]{:S(2)}) collective-permute-start(bf16[32,1280]{1,0:T(8,128)(2,1)S(1)} %collective-permute-done.6.refs_2_), channel_id=1, source_target_pairs={{0,1},{1,0},{2,3},{3,2},{4,5},{5,4},{6,7},{7,6},{8,9},{9,8},{10,11... | collective-permute-start | bytes 245768 | tf_op jit(solution)/shard_map/ppermute | solution.py:472
  22.9 7.7 %collective-permute-start.5 = (bf16[32,1280]{1,0:T(8,128)(2,1)S(1)}, bf16[32,1280]{1,0:T(8,128)(2,1)S(1)}, u32[]{:S(2)}, u32[]{:S(2)}) collective-permute-start(bf16[32,1280]{1,0:T(8,128)(2,1)S(1)} %get-tuple-element.26), channel_id=1, source_target_pairs={{0,28},{4,24},{8,20},{12,16},{16,12},{20,8},{24,4},{28,0},{1,29},{... | collective-permute-start | bytes 245768 | tf_op jit(solution)/shard_map/ppermute | solution.py:466
  24.9 5.6 %collective-permute-start = (s32[2,1,40]{2,1,0:T(1,128)S(1)}, s32[2,1,40]{2,1,0:T(1,128)S(1)}, u32[]{:S(2)}, u32[]{:S(2)}) collective-permute-start(s32[2,1,40]{2,1,0:T(1,128)S(1)} %copy-done.1), channel_id=1, source_target_pairs={{0,2},{1,3},{2,0},{3,1},{4,6},{5,7},{6,4},{7,5},{8,10},{9,11},{10,... | collective-permute-start | bytes 968 | tf_op jit(solution)/shard_map/ppermute | solution.py:461
  25.6 10.6 %collective-permute-start.1 = (bf16[32,1280]{1,0:T(8,128)(2,1)S(1)}, bf16[32,1280]{1,0:T(8,128)(2,1)S(1)}, u32[]{:S(2)}, u32[]{:S(2)}) collective-permute-start(bf16[32,1280]{1,0:T(8,128)(2,1)S(1)} %get-tuple-element.22), channel_id=1, source_target_pairs={{0,20},{4,16},{8,28},{12,24},{16,4},{20,0},{24,12},{28,8},{1,21},{... | collective-permute-start | bytes 245768 | tf_op jit(solution)/shard_map/ppermute | solution.py:466
  27.1 9.0 %collective-permute-start.2 = (bf16[32,1280]{1,0:T(8,128)(2,1)S(1)}, bf16[32,1280]{1,0:T(8,128)(2,1)S(1)}, u32[]{:S(2)}, u32[]{:S(2)}) collective-permute-start(bf16[32,1280]{1,0:T(8,128)(2,1)S(1)} %get-tuple-element.23), channel_id=1, source_target_pairs={{0,24},{4,28},{8,16},{12,20},{16,8},{20,12},{24,0},{28,4},{1,25},{... | collective-permute-start | bytes 245768 | tf_op jit(solution)/shard_map/ppermute | solution.py:466
  30.6 6.1 %collective-permute-start.14 = (bf16[32,1280]{1,0:T(8,128)(2,1)S(1)}, bf16[32,1280]{1,0:T(8,128)(2,1)S(1)}, u32[]{:S(2)}, u32[]{:S(2)}) collective-permute-start(bf16[32,1280]{1,0:T(8,128)(2,1)S(1)} %collective-permute-done.3.refs_1_), channel_id=1, source_target_pairs={{0,1},{1,0},{2,3},{3,2},{4,5},{5,4},{6,7},{7,6},{8,9},{9,8},{10,11... | collective-permute-start | bytes 245768 | tf_op jit(solution)/shard_map/ppermute | solution.py:472
  30.6 6.1 %collective-permute-start.15 = (bf16[32,1280]{1,0:T(8,128)(2,1)S(1)}, bf16[32,1280]{1,0:T(8,128)(2,1)S(1)}, u32[]{:S(2)}, u32[]{:S(2)}) collective-permute-start(bf16[32,1280]{1,0:T(8,128)(2,1)S(1)} %collective-permute-done.4.refs_2_), channel_id=1, source_target_pairs={{0,1},{1,0},{2,3},{3,2},{4,5},{5,4},{6,7},{7,6},{8,9},{9,8},{10,11... | collective-permute-start | bytes 245768 | tf_op jit(solution)/shard_map/ppermute | solution.py:472
  31.1 5.6 %collective-permute-start.16 = (bf16[32,1280]{1,0:T(8,128)(2,1)S(1)}, bf16[32,1280]{1,0:T(8,128)(2,1)S(1)}, u32[]{:S(2)}, u32[]{:S(2)}) collective-permute-start(bf16[32,1280]{1,0:T(8,128)(2,1)S(1)} %collective-permute-done.5.refs_3_), channel_id=1, source_target_pairs={{0,1},{1,0},{2,3},{3,2},{4,5},{5,4},{6,7},{7,6},{8,9},{9,8},{10,11... | collective-permute-start | bytes 245768 | tf_op jit(solution)/shard_map/ppermute | solution.py:472
  36.2 1.8 %collective-permute-start.12 = (bf16[32,1280]{1,0:T(8,128)(2,1)S(1)}, bf16[32,1280]{1,0:T(8,128)(2,1)S(1)}, u32[]{:S(2)}, u32[]{:S(2)}) collective-permute-start(bf16[32,1280]{1,0:T(8,128)(2,1)S(1)} %collective-permute-done.1.refs_1_.refs_4_), channel_id=1, source_target_pairs={{0,1},{1,0},{2,3},{3,2},{4,5},{5,4},{6,7},{7,6},{8,9},{9,8},{10,11... | collective-permute-start | bytes 245768 | tf_op jit(solution)/shard_map/ppermute | solution.py:472
  36.2 1.8 %collective-permute-start.13 = (bf16[32,1280]{1,0:T(8,128)(2,1)S(1)}, bf16[32,1280]{1,0:T(8,128)(2,1)S(1)}, u32[]{:S(2)}, u32[]{:S(2)}) collective-permute-start(bf16[32,1280]{1,0:T(8,128)(2,1)S(1)} %collective-permute-done.2.refs_2_.refs_5_), channel_id=1, source_target_pairs={{0,1},{1,0},{2,3},{3,2},{4,5},{5,4},{6,7},{7,6},{8,9},{9,8},{10,11... | collective-permute-start | bytes 245768 | tf_op jit(solution)/shard_map/ppermute | solution.py:472
  39.1 4.3 %collective-permute-start.17 = (bf16[2,2,16,512]{3,2,1,0:T(8,128)(2,1)S(1)}, bf16[2,2,16,512]{3,2,1,0:T(8,128)(2,1)S(1)}, u32[]{:S(2)}, u32[]{:S(2)}) collective-permute-start(bf16[2,2,16,512]{3,2,1,0:T(8,128)(2,1)S(1)} %coefficients.8), channel_id=1, source_target_pairs={{0,2},{1,3},{2,0},{3,1},{4,6},{5,7},{6,4},{7,5},{8,10},{9,11},{10,... | collective-permute-start | bytes 196616 | tf_op jit(solution)/shard_map/ppermute | solution.py:490
